TPU v7x, 32 devices: a whole 2x2x4 slice. The times are simulated.
32 devices in a mesh: band: 8 (over y, x, core), lev: 4 (over z).
Axes of the slice: x: 2, y: 2, z: 4, core: 2. Of those that a mesh axis runs over, the one named last changes fastest.
Arguments:
- pattern: float32 [1024, 128], P('band'), may hold values from -3 to 3
- taper: float32 [136], P('lev'), may hold values from 0.1 to 1
- thickness: float32 [136], P('lev'), may hold values from 0.2 to 2
- block_source: int32 [1024], P('band'), may hold values from 0 to 1023, as said below
- tendencies: bfloat16 [4, 136, 131072], P(None, 'lev', 'band'), may hold values from -6 to 6
Outputs:
- perturbed: bfloat16 [4, 136, 131072], P(None, 'lev', 'band')
- integrals: float32 [2, 131072], P(None, 'band')
Inputs may be any that keep to these rules, and one draw needn't show every extreme that they name: block_source is a permutation of 0 to 1023; the 128 physics blocks of each band index take exactly 128 // 8 grid blocks from the 128 grid blocks of each band index.
All inputs are finite; a program needn't handle non-finite values.
Results may differ from a plain program's by a relative error of at most 0.001.
Values sent between devices are 32-bit elements; how exact they have to be, the bound alone decides.
A program may use at most 64 MiB of HBM per device.

v0:
```python
import functools
import jax
import jax.numpy as jnp
from jax import lax
from jax.experimental import pallas as pl
from jax.experimental.pallas import tpu as pltpu
from jax.sharding import PartitionSpec as P

MESH = pl.DeviceIdType.MESH


def exchange(n_band, n_lev, pattern, source_hbm, taper_hbm, thickness_hbm, tend, held, spread, totals,
             whole, acc, part, inbox, source, taper, thickness, small_sem, own_sem, load_sem, out_sem, in_sem, pass_sem, got_sem,
             part_send, part_recv, total_send, total_recv):
    band, lev = lax.axis_index("band"), lax.axis_index("lev")
    levels, rows, lanes = tend.shape
    blocks = pattern.shape[0]
    fields = rows // blocks
    pieces, half = totals.shape[0], n_lev // 2
    share, piece = blocks // pieces, rows // pieces
    pairs = n_band // 2
    per = pieces // 2
    side = lev // half
    near, far = half - 1 + side, half - side
    pair, core = band // 2, band % 2
    mate = pair * 2 + 1 - core

    def chunk_of(step):
        owner = 1 - side if step % 2 == 0 else side
        return owner * per + step // 2

    def load(step):
        span = pl.ds(pl.multiple_of(chunk_of(step) * piece, piece), piece)
        return pltpu.make_async_copy(tend.at[:, span, :], held.at[:, span, :], load_sem.at[step])

    def block_rows(who):
        return pl.ds(pl.multiple_of(who * blocks, blocks), blocks)

    own = pltpu.make_async_copy(pattern, whole.at[block_rows(band)], own_sem)
    own.start()
    small = [pltpu.make_async_copy(a, b, small_sem.at[i]) for i, (a, b) in enumerate(
        ((thickness_hbm, thickness), (taper_hbm, taper), (source_hbm, source)))]
    for copy in small:
        copy.start()
    for step in range(pieces):
        load(step).start()

    barrier = pltpu.get_barrier_semaphore()
    pl.semaphore_signal(barrier, inc=1, device_id={"band": mate}, device_id_type=MESH)
    for d in range(1, pairs):
        peer = lax.rem(pair + d, pairs) * 2 + core
        pl.semaphore_signal(barrier, inc=1, device_id={"band": peer}, device_id_type=MESH)
    for d in range(1, n_lev):
        peer = lax.rem(lev + d, n_lev)

        @pl.when((lev == near) | (peer == half - 1) | (peer == half))
        def _(peer=peer):
            pl.semaphore_signal(barrier, inc=1, device_id={"lev": peer}, device_id_type=MESH)

    def direct(d):
        peer = lax.rem(pair + d, pairs) * 2 + core
        mine = whole.at[block_rows(band)]
        return pltpu.make_async_remote_copy(mine, mine, out_sem.at[d], in_sem.at[d],
                                            device_id={"band": peer}, device_id_type=MESH)

    def relay(d):
        origin = lax.rem(pair - d + pairs, pairs) * 2 + core
        block = whole.at[block_rows(origin)]
        return pltpu.make_async_remote_copy(block, block, pass_sem.at[d], got_sem.at[d],
                                            device_id={"band": mate}, device_id_type=MESH)

    for copy in small:
        copy.wait()
    squares = thickness[0] * thickness[0]
    for l in range(1, levels):
        squares += thickness[l] * thickness[l]

    def give(step):
        return pltpu.make_async_remote_copy(part.at[step], inbox.at[lev, step // 2], part_send.at[step],
                                            part_recv.at[lev, step // 2],
                                            device_id={"lev": far if step % 2 == 0 else near}, device_id_type=MESH)

    def got(peer, q):
        return pltpu.make_async_remote_copy(part.at[q], inbox.at[peer, q], part_send.at[q], part_recv.at[peer, q],
                                            device_id={"lev": peer}, device_id_type=MESH)

    def publish(d, q):
        mine = totals.at[side * per + q]
        return pltpu.make_async_remote_copy(mine, mine, total_send.at[d, q], total_recv.at[side * per + q],
                                            device_id={"lev": lax.rem(lev + d, n_lev)}, device_id_type=MESH)

    def send(step):
        if step % 2 == 0:
            give(step).start()
        else:
            pl.when(lev != near)(lambda: give(step).start())

    def level_sums(step):
        load(step).wait()
        first = pl.multiple_of(chunk_of(step) * piece, piece)
        for r in range(0, piece, 64):
            def add(l, total):
                weight = thickness[l] * taper[l]
                return total + weight * held[l, pl.ds(first + r, 64), :].astype(jnp.float32)
            acc[pl.ds(r, 64), :] = lax.fori_loop(0, levels, add, jnp.zeros((64, lanes), jnp.float32), unroll=34)
        for k in range(2):
            part[step, k * share:(k + 1) * share, :] = acc[pl.ds(fields - 2 + k, share, stride=fields), :]
        part[step, 2 * share:, :] = jnp.full((1, lanes), squares, jnp.float32)

    for step in range(2):
        level_sums(step)
    own.wait()
    met = jnp.where(lev == near, n_lev - 1, 2)
    pl.semaphore_wait(barrier, pairs + met)
    for step in range(2):
        send(step)
    for d in range(1, pairs):
        direct(d).start()
    relay(0).start()

    for step in range(2, pieces):
        level_sums(step)
        send(step)

    @pl.when(lev == near)
    def _():
        for q in range(per):
            total = part[2 * q + 1]
            for d in range(1, n_lev):
                peer = lax.rem(lev + d, n_lev)
                got(peer, q).wait_recv()
                total = total + inbox[peer, q]
            totals[side * per + q] = total[:2 * share] / jnp.sqrt(total[2 * share:2 * share + 1])
            for d in range(1, n_lev):
                publish(d, q).start()

    for d in range(1, pairs):
        direct(d).wait_recv()
        relay(d).start()
    for d in range(pairs):
        relay(d).wait()
    for d in range(1, pairs):
        direct(d).wait_send()

    def pick(j, _):
        row = whole[pl.ds(source[j], 1), :]
        acc[pl.ds(j, 1), :] = row
        return 0

    lax.fori_loop(0, blocks, pick, 0, unroll=32)
    local = jnp.tanh(acc[0:blocks, :])
    for f in range(fields):
        spread[pl.ds(f, blocks, stride=fields), :] = local

    for step in range(pieces):
        if step % 2 == 0:
            give(step).wait_send()
        else:
            pl.when(lev != near)(lambda step=step: give(step).wait_send())

    @pl.when(lev == near)
    def _():
        for q in range(per):
            for d in range(1, n_lev):
                publish(d, q).wait_send()

    for p in range(pieces):
        @pl.when(lev != half - 1 + p // per)
        def _(p=p):
            pltpu.make_async_remote_copy(totals.at[p], totals.at[p], total_send.at[0, 0], total_recv.at[p],
                                         device_id={"lev": far}, device_id_type=MESH).wait_recv()


def scale(taper, held, spread, totals, out, column, made, sums, out_sem, sum_sem):
    levels, rows, lanes = held.shape
    blocks = column.shape[0]
    pieces = totals.shape[0]
    share, fields = blocks // pieces, rows // blocks

    def level(l, _):
        for r in range(0, rows, 64):
            factor = 1.0 + taper[l] * spread[pl.ds(r, 64), :]
            made[l, pl.ds(r, 64), :] = (held[l, pl.ds(r, 64), :].astype(jnp.float32) * factor).astype(made.dtype)
        pltpu.make_async_copy(made.at[l], out.at[l], out_sem.at[l]).start()
        return 0

    lax.fori_loop(0, levels, level, 0)
    for c in range(pieces):
        local = spread[pl.ds(c * share * fields, share, stride=fields), :]
        for k in range(2):
            sums[c * share:(c + 1) * share, k, :] = totals[c, k * share:(k + 1) * share, :] * local
    done = pltpu.make_async_copy(sums, column, sum_sem)
    done.start()

    def finish(l, _):
        pltpu.make_async_copy(made.at[l], out.at[l], out_sem.at[l]).wait()
        return 0

    lax.fori_loop(0, levels, finish, 0)
    done.wait()


def body(n_band, n_lev, pattern, taper, thickness, block_source, tendencies):
    fields, levels, columns = tendencies.shape
    blocks, lanes = pattern.shape
    rows = blocks * fields
    pieces = 4
    share, piece, pairs = blocks // pieces, rows // pieces, n_band // 2
    tend = tendencies.transpose(1, 0, 2).reshape(levels, fields, blocks, lanes)
    tend = tend.transpose(0, 2, 1, 3).reshape(levels, rows, lanes)
    anywhere = pl.BlockSpec(memory_space=pl.ANY)
    hbm = pl.BlockSpec(memory_space=pltpu.HBM)
    scalars = pl.BlockSpec(memory_space=pltpu.SMEM)
    vector = pl.BlockSpec(memory_space=pltpu.VMEM)
    f32, dma = jnp.float32, pltpu.SemaphoreType.DMA
    held, spread, totals = pl.pallas_call(
        functools.partial(exchange, n_band, n_lev),
        name="exchange",
        out_shape=(pltpu.VMEM(tend.shape, tend.dtype), pltpu.VMEM((rows, lanes), f32),
                   pltpu.VMEM((pieces, 2 * share, lanes), f32)),
        in_specs=[hbm] * 5,
        out_specs=(vector, vector, vector),
        scratch_shapes=[
            pltpu.VMEM((n_band * blocks, lanes), f32),
            pltpu.VMEM((max(piece, blocks), lanes), f32),
            pltpu.VMEM((pieces, 2 * share + 1, lanes), f32),
            pltpu.VMEM((n_lev, pieces // 2, 2 * share + 1, lanes), f32),
            pltpu.SMEM(block_source.shape, jnp.int32), pltpu.SMEM(taper.shape, f32),
            pltpu.SMEM(thickness.shape, f32), dma((3,)),
            dma, dma((pieces,)), dma((pairs,)), dma((pairs,)), dma((pairs,)), dma((pairs,)),
            dma((pieces,)), dma((n_lev, pieces // 2)), dma((n_lev, pieces // 2)), dma((pieces,)),
        ],
        compiler_params=pltpu.CompilerParams(collective_id=0, has_side_effects=True, vmem_limit_bytes=12 << 20),
    )(*(pltpu.with_memory_space_constraint(x, pltpu.MemorySpace.HBM)
        for x in (pattern, block_source, taper, thickness, tend)))
    in_vmem = lambda x: pltpu.with_memory_space_constraint(x, pltpu.MemorySpace.VMEM)
    out, column = pl.pallas_call(
        scale,
        name="scale",
        out_shape=(jax.ShapeDtypeStruct(tend.shape, tend.dtype), jax.ShapeDtypeStruct((blocks, 2, lanes), f32)),
        in_specs=[scalars, vector, vector, vector],
        out_specs=(anywhere, anywhere),
        scratch_shapes=[pltpu.VMEM(tend.shape, tend.dtype), pltpu.VMEM((blocks, 2, lanes), f32), dma((levels,)), dma],
        compiler_params=pltpu.CompilerParams(vmem_limit_bytes=24 << 20),
    )(taper, in_vmem(held), in_vmem(spread), in_vmem(totals))
    out = out.reshape(levels, blocks, fields, lanes).transpose(2, 0, 1, 3).reshape(fields, levels, columns)
    return out, column.transpose(1, 0, 2).reshape(2, columns)


def solution(mesh):
    in_specs = (P("band", None), P("lev"), P("lev"), P("band"), P(None, "lev", "band"))
    out_specs = (P(None, "lev", "band"), P(None, "band"))
    run = functools.partial(body, mesh.shape["band"], mesh.shape["lev"])
    return jax.shard_map(run, mesh=mesh, in_specs=in_specs, out_specs=out_specs, check_vma=False)
```

profile of v0, /device:TPU:0, one launch (start us, length us, event | category | flops | bytes accessed | tf_op | source)
XLA Modules:
  0.0 17.5 jit_solution(6873664721728695514)
XLA Ops:
  0.6 0.0 copy-start
  0.6 13.8 %exchange.1 = (bf16[34,512,128]{2,1,0:T(8,128)(2,1)S(1)}, f32[512,128]{1,0:T(8,128)S(1)}, f32[4,64,128]{2,1,0:T(8,128)S(1)}) custom-call(f32[128,128]{1,0:T(8,128)} %pattern.1, s32[128]{0:T(128)} %source_hbm.1, f32[34]{0:T(128)} %taper.1, f32[34]{0:T(128)} %thickness_hbm.1, bf16[34,512,128]{2,1,0:T(8,128)(2,1)} %bitcast.15), custom_call_target="tpu_custom_call" | custom-call | tf_op jit(solution)/shard_map/exchange/pallas_call | solution.py:216
  14.4 0.0 copy-done
  14.4 3.1 %scale.1 = (bf16[34,512,128]{2,1,0:T(8,128)(2,1)}, f32[128,2,128]{2,1,0:T(2,128)}) custom-call(f32[34]{0:T(128)S(1)} %copy-done, bf16[34,512,128]{2,1,0:T(8,128)(2,1)S(1)} %get-tuple-element.7.held, f32[512,128]{1,0:T(8,128)S(1)} %get-tuple-element.8.spread, f32[4,64,128]{2,1,0:T(8,128)S(1)} %get-tuple-element.9.totals), custom_call_target="tpu_custom_call" | custom-call | tf_op jit(solution)/shard_map/scale/pallas_call | solution.py:237
Async XLA Ops:
  0.6 13.8 %copy-start = (f32[34]{0:T(128)S(1)}, f32[34]{0:T(128)}, u32[]{:S(2)}) copy-start(f32[34]{0:T(128)} %taper.1) | copy-start | bytes 412
where the time goes:
time: 17.7 us; the launch traced here: 17.5 us
  Pallas kernels  16.9 us (95%)
  between operations  0.65 us (4%)
    pallas_call x1, Pallas kernels, body(): pl.pallas_call(functools.partial(exchange, n_band, n_lev), name='exchange...  13.8 us
    pallas_call x1, Pallas kernels, body(): pl.pallas_call(scale, name='scale', out_shape=(jax.ShapeDtypeStruct(tend....  3.1 us

commit v1 on v0

v1 whole, which is shorter than its diff:
```python
import functools
import jax
import jax.numpy as jnp
from jax import lax
from jax.experimental import pallas as pl
from jax.experimental.pallas import tpu as pltpu
from jax.sharding import PartitionSpec as P

MESH = pl.DeviceIdType.MESH


def exchange(n_band, n_lev, pattern, source_hbm, taper_hbm, thickness_hbm, tend, made, sums,
             held, spread, whole, acc, part, inbox, totals, partial, outgoing, source, taper, thickness,
             small_sem, own_sem, load_sem, ready, mate_ready, lev_ready, out_sem, in_sem, pass_sem,
             part_send, part_recv, partial_send, total_send, total_recv):
    band, lev = lax.axis_index("band"), lax.axis_index("lev")
    levels, rows, lanes = tend.shape
    blocks = pattern.shape[0]
    fields = rows // blocks
    pieces, half = totals.shape[0], n_lev // 2
    share, piece = blocks // pieces, rows // pieces
    pairs = n_band // 2
    per = pieces // 2
    side = lev // half
    near, far = half - 1 + side, half - side
    pair, core = band // 2, band % 2
    hub, keeper = core == 0, 2 * pair + 1
    owner = (core == 1) & (lev == near)

    def signal(sem, **where):
        pl.semaphore_signal(sem, inc=1, device_id=where, device_id_type=MESH)

    def block_rows(who):
        return pl.ds(pl.multiple_of(who * blocks, blocks), blocks)

    barrier = pltpu.get_barrier_semaphore()
    for t in range(half - 1, half + 1):
        pl.when(lev < t)(lambda t=t: signal(barrier, band=keeper, lev=t))
    for t in range(half, n_lev):
        @pl.when(owner & (lev < t))
        def _(t=t):
            signal(barrier, band=2 * pair, lev=t)
            if t > half:
                signal(barrier, band=keeper, lev=t)
    pl.when(hub)(lambda: signal(barrier, band=keeper))
    for t in range(1, pairs):
        @pl.when(pair < t)
        def _(t=t):
            signal(barrier, band=2 * t)
            pl.when(hub)(lambda: signal(barrier, band=2 * t + 1))
    from_band = jnp.where(hub, 2 * pair, pair + 1)
    from_lev = jnp.where(lev > half, 2, jnp.where(hub, lev // half, jnp.where(lev < half - 1, 0, 2 * lev)))
    expected = from_band + from_lev

    own = pltpu.make_async_copy(pattern, whole.at[block_rows(band)], own_sem)
    own.start()
    small = [pltpu.make_async_copy(a, b, small_sem.at[i]) for i, (a, b) in enumerate(
        ((thickness_hbm, thickness), (taper_hbm, taper), (source_hbm, source)))]
    for copy in small:
        copy.start()

    def chunk_of(step):
        return (1 - side if step % 2 == 0 else side) * per + step // 2

    def load(step):
        span = pl.ds(pl.multiple_of(chunk_of(step) * piece, piece), piece)
        return pltpu.make_async_copy(tend.at[:, span, :], held.at[:, span, :], load_sem.at[step])

    for step in range(pieces):
        load(step).start()

    def direct(t):
        mine = whole.at[block_rows(band)]
        return pltpu.make_async_remote_copy(mine, mine, out_sem.at[t], in_sem.at[band],
                                            device_id={"band": 2 * t}, device_id_type=MESH)

    def relay(origin):
        block = whole.at[block_rows(origin)]
        return pltpu.make_async_remote_copy(block, block, pass_sem.at[origin], in_sem.at[origin],
                                            device_id={"band": keeper}, device_id_type=MESH)

    def came(origin):
        block = whole.at[block_rows(origin)]
        pltpu.make_async_remote_copy(block, block, pass_sem.at[origin], in_sem.at[origin],
                                     device_id={"band": band + 1 - 2 * core}, device_id_type=MESH).wait_recv()

    def give(step):
        where = {"band": keeper, "lev": far if step % 2 == 0 else near}
        return pltpu.make_async_remote_copy(part.at[step], inbox.at[core, lev, step // 2], part_send.at[step],
                                            part_recv.at[core, lev, step // 2],
                                            device_id=where, device_id_type=MESH)

    def got(c, e, q):
        pltpu.make_async_remote_copy(part.at[q], inbox.at[c, e, q], part_send.at[q], part_recv.at[c, e, q],
                                     device_id={"lev": far}, device_id_type=MESH).wait_recv()

    def publish_first(c, q):
        return pltpu.make_async_remote_copy(partial.at[c, q], totals.at[side * per + q], partial_send.at[c, q],
                                            total_recv.at[side * per + q],
                                            device_id={"band": 2 * pair + c, "lev": 0}, device_id_type=MESH)

    def publish(c, t, q):
        return pltpu.make_async_remote_copy(outgoing.at[c, q], totals.at[side * per + q], total_send.at[c, t, q],
                                            total_recv.at[side * per + q],
                                            device_id={"band": 2 * pair + c, "lev": t}, device_id_type=MESH)

    def elsewhere(c, t):
        return True if c == 0 else lev != t

    pl.when(expected > 0)(lambda: pl.semaphore_wait(barrier, expected))
    for t in range(half):
        @pl.when(owner & (lev > t))
        def _(t=t):
            signal(lev_ready.at[side], band=2 * pair, lev=t)
            signal(lev_ready.at[side], band=keeper, lev=t)
    pl.when(core == 1)(lambda: signal(mate_ready, band=2 * pair))
    for t in range(pairs - 1):
        @pl.when(hub & (pair > t))
        def _(t=t):
            signal(ready.at[pair], band=2 * t)
            signal(ready.at[pair], band=2 * t + 1)
    own.wait()
    for t in range(pairs):
        pl.when((pair > t) | ((core == 1) & (pair == t)))(lambda t=t: direct(t).start())

    for copy in small:
        copy.wait()
    squares = thickness[0] * thickness[0]
    for l in range(1, levels):
        squares += thickness[l] * thickness[l]
    pl.when(hub)(lambda: pl.semaphore_wait(mate_ready, 1))
    for step in range(pieces):
        load(step).wait()
        first = pl.multiple_of(chunk_of(step) * piece, piece)
        for r in range(0, piece, 64):
            def add(l, total):
                weight = thickness[l] * taper[l]
                return total + weight * held[l, pl.ds(first + r, 64), :].astype(jnp.float32)
            acc[pl.ds(r, 64), :] = lax.fori_loop(0, levels, add, jnp.zeros((64, lanes), jnp.float32), unroll=34)
        for k in range(2):
            part[step, k * share:(k + 1) * share, :] = acc[pl.ds(fields - 2 + k, share, stride=fields), :]
        part[step, 2 * share:, :] = jnp.full((1, lanes), squares, jnp.float32)
        if step == 0:
            pl.when(lev < half)(lambda: pl.semaphore_wait(lev_ready.at[1], 1))
            give(step).start()
        elif step == 1:
            pl.when(lev < half - 1)(lambda: pl.semaphore_wait(lev_ready.at[0], 1))
        if step % 2 == 0:
            if step:
                give(step).start()
        else:
            pl.when(jnp.logical_not(owner))(lambda step=step: give(step).start())
    for t in range(1, pairs):
        @pl.when(pair < t)
        def _(t=t):
            pl.semaphore_wait(ready.at[t], 1)
            direct(t).start()

    @pl.when(owner)
    def _():
        for q in range(per):
            inbox[1, lev, q] = part[2 * q + 1]
        for c in (1, 0):
            for q in range(per):
                for e in range(1, n_lev):
                    pl.when(elsewhere(c, e))(lambda c=c, e=e, q=q: got(c, e, q))
                total = inbox[c, 1, q]
                for e in range(2, n_lev):
                    total = total + inbox[c, e, q]
                partial[c, q] = total
                publish_first(c, q).start()
        for c in (1, 0):
            for q in range(per):
                got(c, 0, q)
                total = inbox[c, 0, q] + partial[c, q]
                outgoing[c, q] = total
                if c == 1:
                    totals[side * per + q] = total
                for t in reversed(range(1, n_lev)):
                    pl.when(elsewhere(c, t))(lambda c=c, t=t, q=q: publish(c, t, q).start())

    @pl.when(hub)
    def _():
        relay(band).start()
        for c in range(2):
            for t in range(pairs):
                @pl.when(pair != t)
                def _(t=t, c=c):
                    came(2 * t + c)
                    relay(2 * t + c).start()
        came(band + 1)

    @pl.when(core == 1)
    def _():
        came(band - 1)
        for c in range(2):
            for t in range(pairs):
                pl.when(pair != t)(lambda t=t, c=c: came(2 * t + c))

    def pick(j, _):
        row = whole[pl.ds(source[j], 1), :]
        spread[pl.ds(pl.multiple_of(j * fields, fields), fields), :] = jnp.broadcast_to(row, (fields, lanes))
        return 0

    lax.fori_loop(0, blocks, pick, 0, unroll=32)

    def scale(i, _):
        span = pl.ds(pl.multiple_of(i * 64, 64), 64)
        local = jnp.tanh(spread[span, :])
        spread[span, :] = local

        def level(l, _):
            made[l, span, :] = (held[l, span, :].astype(jnp.float32) * (1.0 + taper[l] * local)).astype(made.dtype)
            return 0

        return lax.fori_loop(0, levels, level, 0, unroll=34)

    lax.fori_loop(0, rows // 64, scale, 0)

    for c in range(pieces):
        @pl.when(jnp.logical_not(owner & (side == c // per)))
        def _(c=c):
            pltpu.make_async_remote_copy(totals.at[c], totals.at[c], total_send.at[0, 0, 0], total_recv.at[c],
                                         device_id={"lev": far}, device_id_type=MESH).wait_recv()

        @pl.when(lev == 0)
        def _(c=c):
            totals[c] = part[2 * (c % per) + 1 - c // per] + totals[c]

        scaled = 1.0 / jnp.sqrt(totals[c, 2 * share:2 * share + 1, :])
        local = spread[pl.ds(c * share * fields, share, stride=fields), :] * scaled
        for k in range(2):
            sums[pl.ds(c * 2 * share + k, share, stride=2), :] = totals[c, k * share:(k + 1) * share, :] * local

    for step in range(pieces):
        if step % 2 == 0:
            give(step).wait_send()
        else:
            pl.when(jnp.logical_not(owner))(lambda step=step: give(step).wait_send())

    @pl.when(owner)
    def _():
        for c in range(2):
            for q in range(per):
                publish_first(c, q).wait_send()
                for t in range(1, n_lev):
                    pl.when(elsewhere(c, t))(lambda c=c, t=t, q=q: publish(c, t, q).wait_send())

    for t in range(pairs):
        pl.when((core == 1) | (pair != t))(lambda t=t: direct(t).wait_send())

    @pl.when(hub)
    def _():
        relay(band).wait_send()
        for c in range(2):
            for t in range(pairs):
                pl.when(pair != t)(lambda t=t, c=c: relay(2 * t + c).wait_send())


def write(made, sums, out, column, out_sem, sum_sem):
    copies = (pltpu.make_async_copy(made, out, out_sem), pltpu.make_async_copy(sums, column, sum_sem))
    for copy in copies:
        copy.start()
    for copy in copies:
        copy.wait()


def body(n_band, n_lev, pattern, taper, thickness, block_source, tendencies):
    assert n_lev == 4 and n_band % 2 == 0
    fields, levels, columns = tendencies.shape
    blocks, lanes = pattern.shape
    rows = blocks * fields
    pieces = 4
    share, piece, pairs = blocks // pieces, rows // pieces, n_band // 2
    per = pieces // 2
    tend = tendencies.transpose(1, 0, 2).reshape(levels, fields, blocks, lanes)
    tend = tend.transpose(0, 2, 1, 3).reshape(levels, rows, lanes)
    hbm = pl.BlockSpec(memory_space=pltpu.HBM)
    vector = pl.BlockSpec(memory_space=pltpu.VMEM)
    f32, dma, flag = jnp.float32, pltpu.SemaphoreType.DMA, pltpu.SemaphoreType.REGULAR
    made, sums = pl.pallas_call(
        functools.partial(exchange, n_band, n_lev),
        name="exchange",
        out_shape=(pltpu.VMEM(tend.shape, tend.dtype), pltpu.VMEM((2 * blocks, lanes), f32)),
        in_specs=[hbm] * 5,
        out_specs=(vector, vector),
        scratch_shapes=[
            pltpu.VMEM(tend.shape, tend.dtype),
            pltpu.VMEM((rows, lanes), f32),
            pltpu.VMEM((n_band * blocks, lanes), f32),
            pltpu.VMEM((piece, lanes), f32),
            pltpu.VMEM((pieces, 2 * share + 1, lanes), f32),
            pltpu.VMEM((2, n_lev, per, 2 * share + 1, lanes), f32),
            pltpu.VMEM((pieces, 2 * share + 1, lanes), f32),
            pltpu.VMEM((2, per, 2 * share + 1, lanes), f32),
            pltpu.VMEM((2, per, 2 * share + 1, lanes), f32),
            pltpu.SMEM(block_source.shape, jnp.int32), pltpu.SMEM(taper.shape, f32), pltpu.SMEM(thickness.shape, f32),
            dma((3,)), dma, dma((pieces,)),
            flag((pairs,)), flag, flag((2,)),
            dma((pairs,)), dma((n_band,)), dma((n_band,)),
            dma((pieces,)), dma((2, n_lev, per)), dma((2, per)), dma((2, n_lev, per)), dma((pieces,)),
        ],
        compiler_params=pltpu.CompilerParams(collective_id=0, has_side_effects=True, vmem_limit_bytes=24 << 20),
    )(*(pltpu.with_memory_space_constraint(x, pltpu.MemorySpace.HBM)
        for x in (pattern, block_source, taper, thickness, tend)))
    in_vmem = lambda x: pltpu.with_memory_space_constraint(x, pltpu.MemorySpace.VMEM)
    out, column = pl.pallas_call(
        write,
        name="write",
        out_shape=(jax.ShapeDtypeStruct(tend.shape, tend.dtype), jax.ShapeDtypeStruct((2 * blocks, lanes), f32)),
        in_specs=[vector, vector],
        out_specs=(hbm, hbm),
        scratch_shapes=[dma, dma],
        compiler_params=pltpu.CompilerParams(vmem_limit_bytes=1 << 20),
    )(in_vmem(made), in_vmem(sums))
    out = out.reshape(levels, blocks, fields, lanes).transpose(2, 0, 1, 3).reshape(fields, levels, columns)
    return out, column.reshape(blocks, 2, lanes).transpose(1, 0, 2).reshape(2, columns)


def solution(mesh):
    in_specs = (P("band", None), P("lev"), P("lev"), P("band"), P(None, "lev", "band"))
    out_specs = (P(None, "lev", "band"), P(None, "band"))
    run = functools.partial(body, mesh.shape["band"], mesh.shape["lev"])
    return jax.shard_map(run, mesh=mesh, in_specs=in_specs, out_specs=out_specs, check_vma=False)
```

time: 17.7 us -> 16.8 us (0.949)
  Pallas kernels: 16.9 us -> 16 us
    pallas_call x1, Pallas kernels: 3.1 us -> 2.14 us  [body(): pl.pallas_call(write, name='write', out_shape=(jax.ShapeDtypeStruct(tend....]
where the time goes in v1:
time: 16.8 us; the launch traced here: 16.6 us
  Pallas kernels  16 us (95%)
  between operations  0.64 us (4%)
    pallas_call x1, Pallas kernels, body(): pl.pallas_call(functools.partial(exchange, n_band, n_lev), name='exchange...  13.8 us
    pallas_call x1, Pallas kernels, body(): pl.pallas_call(write, name='write', out_shape=(jax.ShapeDtypeStruct(tend....  2.14 us

profile of v1, /device:TPU:0, one launch (start us, length us, event | category | flops | bytes accessed | tf_op | source)
XLA Modules:
  0.0 16.6 jit_solution(7183649884153336716)
XLA Ops:
  0.6 13.8 %exchange.1 = (bf16[34,512,128]{2,1,0:T(8,128)(2,1)S(1)}, f32[256,128]{1,0:T(8,128)S(1)}) custom-call(f32[128,128]{1,0:T(8,128)} %pattern.1, s32[128]{0:T(128)} %source_hbm.1, f32[34]{0:T(128)} %taper_hbm.1, f32[34]{0:T(128)} %thickness_hbm.1, bf16[34,512,128]{2,1,0:T(8,128)(2,1)} %bitcast.17), custom_call_target="tpu_custom_call" | custom-call | tf_op jit(solution)/shard_map/exchange/pallas_call | solution.py:281
  14.5 2.1 %write.1 = (bf16[34,512,128]{2,1,0:T(8,128)(2,1)}, f32[256,128]{1,0:T(8,128)}) custom-call(bf16[34,512,128]{2,1,0:T(8,128)(2,1)S(1)} %get-tuple-element.6.made, f32[256,128]{1,0:T(8,128)S(1)} %get-tuple-element.7.sums), custom_call_target="tpu_custom_call" | custom-call | tf_op jit(solution)/shard_map/write/pallas_call | solution.py:307

commit v2 on v1

--- a/solution.py
+++ b/solution.py
@@ -11,8 +11,7 @@
 
 def exchange(n_band, n_lev, pattern, source_hbm, taper_hbm, thickness_hbm, tend, made, sums,
              held, spread, whole, acc, part, inbox, totals, partial, outgoing, source, taper, thickness,
-             small_sem, own_sem, load_sem, ready, mate_ready, lev_ready, out_sem, in_sem, pass_sem,
-             part_send, part_recv, partial_send, total_send, total_recv):
+             small_sem, own_sem, load_sem, ready, mate_ready, lev_ready, in_sem, part_recv, total_recv):
     band, lev = lax.axis_index("band"), lax.axis_index("lev")
     levels, rows, lanes = tend.shape
     blocks = pattern.shape[0]
@@ -26,6 +25,7 @@
     pair, core = band // 2, band % 2
     hub, keeper = core == 0, 2 * pair + 1
     owner = (core == 1) & (lev == near)
+    out_sem, pass_sem, part_send, publish_send = own_sem, small_sem.at[0], small_sem.at[1], load_sem
 
     def signal(sem, **where):
         pl.semaphore_signal(sem, inc=1, device_id=where, device_id_type=MESH)
@@ -71,37 +71,33 @@
 
     def direct(t):
         mine = whole.at[block_rows(band)]
-        return pltpu.make_async_remote_copy(mine, mine, out_sem.at[t], in_sem.at[band],
+        return pltpu.make_async_remote_copy(mine, mine, out_sem, in_sem.at[band],
                                             device_id={"band": 2 * t}, device_id_type=MESH)
 
     def relay(origin):
         block = whole.at[block_rows(origin)]
-        return pltpu.make_async_remote_copy(block, block, pass_sem.at[origin], in_sem.at[origin],
+        return pltpu.make_async_remote_copy(block, block, pass_sem, in_sem.at[0],
                                             device_id={"band": keeper}, device_id_type=MESH)
 
+    def remote(ref, send, receive):
+        return pltpu.make_async_remote_copy(ref, ref, send, receive,
+                                            device_id={"lev": far}, device_id_type=MESH)
+
     def came(origin):
-        block = whole.at[block_rows(origin)]
-        pltpu.make_async_remote_copy(block, block, pass_sem.at[origin], in_sem.at[origin],
-                                     device_id={"band": band + 1 - 2 * core}, device_id_type=MESH).wait_recv()
+        remote(whole.at[block_rows(origin)], pass_sem, in_sem.at[origin]).wait_recv()
 
     def give(step):
         where = {"band": keeper, "lev": far if step % 2 == 0 else near}
-        return pltpu.make_async_remote_copy(part.at[step], inbox.at[core, lev, step // 2], part_send.at[step],
-                                            part_recv.at[core, lev, step // 2],
+        return pltpu.make_async_remote_copy(part.at[step], inbox.at[core, step // 2, lev], part_send,
+                                            part_recv.at[core, jnp.where(lev == 0, per, step // 2)],
                                             device_id=where, device_id_type=MESH)
 
-    def got(c, e, q):
-        pltpu.make_async_remote_copy(part.at[q], inbox.at[c, e, q], part_send.at[q], part_recv.at[c, e, q],
-                                     device_id={"lev": far}, device_id_type=MESH).wait_recv()
-
     def publish_first(c, q):
-        return pltpu.make_async_remote_copy(partial.at[c, q], totals.at[side * per + q], partial_send.at[c, q],
-                                            total_recv.at[side * per + q],
+        return pltpu.make_async_remote_copy(partial.at[c, q], totals.at[side * per + q], publish_send.at[c], total_recv,
                                             device_id={"band": 2 * pair + c, "lev": 0}, device_id_type=MESH)
 
     def publish(c, t, q):
-        return pltpu.make_async_remote_copy(outgoing.at[c, q], totals.at[side * per + q], total_send.at[c, t, q],
-                                            total_recv.at[side * per + q],
+        return pltpu.make_async_remote_copy(outgoing.at[c, q], totals.at[side * per + q], publish_send.at[c], total_recv,
                                             device_id={"band": 2 * pair + c, "lev": t}, device_id_type=MESH)
 
     def elsewhere(c, t):
@@ -111,14 +107,14 @@
     for t in range(half):
         @pl.when(owner & (lev > t))
         def _(t=t):
-            signal(lev_ready.at[side], band=2 * pair, lev=t)
-            signal(lev_ready.at[side], band=keeper, lev=t)
+            signal(lev_ready, band=2 * pair, lev=t)
+            signal(lev_ready, band=keeper, lev=t)
     pl.when(core == 1)(lambda: signal(mate_ready, band=2 * pair))
     for t in range(pairs - 1):
         @pl.when(hub & (pair > t))
         def _(t=t):
-            signal(ready.at[pair], band=2 * t)
-            signal(ready.at[pair], band=2 * t + 1)
+            signal(ready, band=2 * t)
+            signal(ready, band=2 * t + 1)
     own.wait()
     for t in range(pairs):
         pl.when((pair > t) | ((core == 1) & (pair == t)))(lambda t=t: direct(t).start())
@@ -141,38 +137,31 @@
             part[step, k * share:(k + 1) * share, :] = acc[pl.ds(fields - 2 + k, share, stride=fields), :]
         part[step, 2 * share:, :] = jnp.full((1, lanes), squares, jnp.float32)
         if step == 0:
-            pl.when(lev < half)(lambda: pl.semaphore_wait(lev_ready.at[1], 1))
+            pl.when(lev < half)(lambda: pl.semaphore_wait(lev_ready, jnp.where(lev < half - 1, 2, 1)))
+        if step % 2 == 0:
             give(step).start()
-        elif step == 1:
-            pl.when(lev < half - 1)(lambda: pl.semaphore_wait(lev_ready.at[0], 1))
-        if step % 2 == 0:
-            if step:
-                give(step).start()
         else:
             pl.when(jnp.logical_not(owner))(lambda step=step: give(step).start())
+    pl.when(pair < pairs - 1)(lambda: pl.semaphore_wait(ready, pairs - 1 - pair))
     for t in range(1, pairs):
-        @pl.when(pair < t)
-        def _(t=t):
-            pl.semaphore_wait(ready.at[t], 1)
-            direct(t).start()
+        pl.when(pair < t)(lambda t=t: direct(t).start())
 
     @pl.when(owner)
     def _():
         for q in range(per):
-            inbox[1, lev, q] = part[2 * q + 1]
+            inbox[1, q, lev] = part[2 * q + 1]
         for c in (1, 0):
             for q in range(per):
-                for e in range(1, n_lev):
-                    pl.when(elsewhere(c, e))(lambda c=c, e=e, q=q: got(c, e, q))
-                total = inbox[c, 1, q]
+                remote(inbox.at[c, q, pl.ds(1, n_lev - 1 - c)], part_send, part_recv.at[c, q]).wait_recv()
+                total = inbox[c, q, 1]
                 for e in range(2, n_lev):
-                    total = total + inbox[c, e, q]
+                    total = total + inbox[c, q, e]
                 partial[c, q] = total
                 publish_first(c, q).start()
         for c in (1, 0):
+            remote(inbox.at[c, :, 0], part_send, part_recv.at[c, per]).wait_recv()
             for q in range(per):
-                got(c, 0, q)
-                total = inbox[c, 0, q] + partial[c, q]
+                total = inbox[c, q, 0] + partial[c, q]
                 outgoing[c, q] = total
                 if c == 1:
                     totals[side * per + q] = total
@@ -192,10 +181,7 @@
 
     @pl.when(core == 1)
     def _():
-        came(band - 1)
-        for c in range(2):
-            for t in range(pairs):
-                pl.when(pair != t)(lambda t=t, c=c: came(2 * t + c))
+        remote(whole.at[pl.ds(0, (n_band - 1) * blocks)], pass_sem, in_sem.at[0]).wait_recv()
 
     def pick(j, _):
         row = whole[pl.ds(source[j], 1), :]
@@ -217,12 +203,9 @@
 
     lax.fori_loop(0, rows // 64, scale, 0)
 
+    pl.when(owner)(lambda: remote(totals.at[pl.ds(0, per)], part_send, total_recv).wait_recv())
+    pl.when(jnp.logical_not(owner))(lambda: remote(totals, part_send, total_recv).wait_recv())
     for c in range(pieces):
-        @pl.when(jnp.logical_not(owner & (side == c // per)))
-        def _(c=c):
-            pltpu.make_async_remote_copy(totals.at[c], totals.at[c], total_send.at[0, 0, 0], total_recv.at[c],
-                                         device_id={"lev": far}, device_id_type=MESH).wait_recv()
-
         @pl.when(lev == 0)
         def _(c=c):
             totals[c] = part[2 * (c % per) + 1 - c // per] + totals[c]
@@ -232,29 +215,20 @@
         for k in range(2):
             sums[pl.ds(c * 2 * share + k, share, stride=2), :] = totals[c, k * share:(k + 1) * share, :] * local
 
-    for step in range(pieces):
-        if step % 2 == 0:
-            give(step).wait_send()
-        else:
-            pl.when(jnp.logical_not(owner))(lambda step=step: give(step).wait_send())
-
     @pl.when(owner)
     def _():
+        remote(part.at[pl.ds(0, per)], part_send, total_recv).wait_send()
         for c in range(2):
-            for q in range(per):
-                publish_first(c, q).wait_send()
-                for t in range(1, n_lev):
-                    pl.when(elsewhere(c, t))(lambda c=c, t=t, q=q: publish(c, t, q).wait_send())
-
-    for t in range(pairs):
-        pl.when((core == 1) | (pair != t))(lambda t=t: direct(t).wait_send())
+            remote(inbox.at[c, :, pl.ds(0, n_lev - c)], publish_send.at[c], total_recv).wait_send()
+
+    pl.when(jnp.logical_not(owner))(lambda: remote(part, part_send, total_recv).wait_send())
 
     @pl.when(hub)
     def _():
-        relay(band).wait_send()
-        for c in range(2):
-            for t in range(pairs):
-                pl.when(pair != t)(lambda t=t, c=c: relay(2 * t + c).wait_send())
+        remote(whole.at[pl.ds(0, (pairs - 1) * blocks)], out_sem, total_recv).wait_send()
+        remote(whole.at[pl.ds(0, (n_band - 1) * blocks)], pass_sem, total_recv).wait_send()
+
+    pl.when(core == 1)(lambda: remote(whole.at[pl.ds(0, pairs * blocks)], out_sem, total_recv).wait_send())
 
 
 def write(made, sums, out, column, out_sem, sum_sem):
@@ -290,15 +264,13 @@
             pltpu.VMEM((n_band * blocks, lanes), f32),
             pltpu.VMEM((piece, lanes), f32),
             pltpu.VMEM((pieces, 2 * share + 1, lanes), f32),
-            pltpu.VMEM((2, n_lev, per, 2 * share + 1, lanes), f32),
+            pltpu.VMEM((2, per, n_lev, 2 * share + 1, lanes), f32),
             pltpu.VMEM((pieces, 2 * share + 1, lanes), f32),
             pltpu.VMEM((2, per, 2 * share + 1, lanes), f32),
             pltpu.VMEM((2, per, 2 * share + 1, lanes), f32),
             pltpu.SMEM(block_source.shape, jnp.int32), pltpu.SMEM(taper.shape, f32), pltpu.SMEM(thickness.shape, f32),
             dma((3,)), dma, dma((pieces,)),
-            flag((pairs,)), flag, flag((2,)),
-            dma((pairs,)), dma((n_band,)), dma((n_band,)),
-            dma((pieces,)), dma((2, n_lev, per)), dma((2, per)), dma((2, n_lev, per)), dma((pieces,)),
+            flag, flag, flag, dma((n_band,)), dma((2, per + 1)), dma,
         ],
         compiler_params=pltpu.CompilerParams(collective_id=0, has_side_effects=True, vmem_limit_bytes=24 << 20),
     )(*(pltpu.with_memory_space_constraint(x, pltpu.MemorySpace.HBM)

time: 16.8 us -> 16.3 us (0.970)
  Pallas kernels: 16 us -> 15.5 us
    pallas_call x1, Pallas kernels: 13.8 us -> 13.3 us  [body(): pl.pallas_call(functools.partial(exchange, n_band, n_lev), name='exchange...]
where the time goes in v2:
time: 16.3 us; the launch traced here: 16.1 us
  Pallas kernels  15.5 us (95%)
  between operations  0.64 us (4%)
    pallas_call x1, Pallas kernels, body(): pl.pallas_call(functools.partial(exchange, n_band, n_lev), name='exchange...  13.3 us
    pallas_call x1, Pallas kernels, body(): pl.pallas_call(write, name='write', out_shape=(jax.ShapeDtypeStruct(tend....  2.14 us

profile of v2, /device:TPU:0, one launch (start us, length us, event | category | flops | bytes accessed | tf_op | source)
XLA Modules:
  0.0 16.1 jit_solution(13926322347291899039)
XLA Ops:
  0.6 13.3 %exchange.1 = (bf16[34,512,128]{2,1,0:T(8,128)(2,1)S(1)}, f32[256,128]{1,0:T(8,128)S(1)}) custom-call(f32[128,128]{1,0:T(8,128)} %pattern.1, s32[128]{0:T(128)} %source_hbm.1, f32[34]{0:T(128)} %taper_hbm.1, f32[34]{0:T(128)} %thickness_hbm.1, bf16[34,512,128]{2,1,0:T(8,128)(2,1)} %bitcast.17), custom_call_target="tpu_custom_call" | custom-call | tf_op jit(solution)/shard_map/exchange/pallas_call | solution.py:255
  14.0 2.1 %write.1 = (bf16[34,512,128]{2,1,0:T(8,128)(2,1)}, f32[256,128]{1,0:T(8,128)}) custom-call(bf16[34,512,128]{2,1,0:T(8,128)(2,1)S(1)} %get-tuple-element.6.made, f32[256,128]{1,0:T(8,128)S(1)} %get-tuple-element.7.sums), custom_call_target="tpu_custom_call" | custom-call | tf_op jit(solution)/shard_map/write/pallas_call | solution.py:279

commit v3 on v2

--- a/solution.py
+++ b/solution.py
@@ -11,7 +11,7 @@
 
 def exchange(n_band, n_lev, pattern, source_hbm, taper_hbm, thickness_hbm, tend, made, sums,
              held, spread, whole, acc, part, inbox, totals, partial, outgoing, source, taper, thickness,
-             small_sem, own_sem, load_sem, ready, mate_ready, lev_ready, in_sem, part_recv, total_recv):
+             small_sem, own_sem, load_sem, ready, mate_ready, lev_ready, in_sem, total_recv):
     band, lev = lax.axis_index("band"), lax.axis_index("lev")
     levels, rows, lanes = tend.shape
     blocks = pattern.shape[0]
@@ -33,25 +33,6 @@
     def block_rows(who):
         return pl.ds(pl.multiple_of(who * blocks, blocks), blocks)
 
-    barrier = pltpu.get_barrier_semaphore()
-    for t in range(half - 1, half + 1):
-        pl.when(lev < t)(lambda t=t: signal(barrier, band=keeper, lev=t))
-    for t in range(half, n_lev):
-        @pl.when(owner & (lev < t))
-        def _(t=t):
-            signal(barrier, band=2 * pair, lev=t)
-            if t > half:
-                signal(barrier, band=keeper, lev=t)
-    pl.when(hub)(lambda: signal(barrier, band=keeper))
-    for t in range(1, pairs):
-        @pl.when(pair < t)
-        def _(t=t):
-            signal(barrier, band=2 * t)
-            pl.when(hub)(lambda: signal(barrier, band=2 * t + 1))
-    from_band = jnp.where(hub, 2 * pair, pair + 1)
-    from_lev = jnp.where(lev > half, 2, jnp.where(hub, lev // half, jnp.where(lev < half - 1, 0, 2 * lev)))
-    expected = from_band + from_lev
-
     own = pltpu.make_async_copy(pattern, whole.at[block_rows(band)], own_sem)
     own.start()
     small = [pltpu.make_async_copy(a, b, small_sem.at[i]) for i, (a, b) in enumerate(
@@ -66,7 +47,29 @@
         span = pl.ds(pl.multiple_of(chunk_of(step) * piece, piece), piece)
         return pltpu.make_async_copy(tend.at[:, span, :], held.at[:, span, :], load_sem.at[step])
 
-    for step in range(pieces):
+    barrier = pltpu.get_barrier_semaphore()
+    for t in range(half - 1, half + 1):
+        pl.when(lev < t)(lambda t=t: signal(barrier, band=keeper, lev=t))
+    for t in range(half, n_lev):
+        @pl.when(owner & (lev < t))
+        def _(t=t):
+            signal(barrier, band=2 * pair, lev=t)
+            if t > half:
+                signal(barrier, band=keeper, lev=t)
+    for step in range(1):
+        load(step).start()
+
+    pl.when(hub)(lambda: signal(barrier, band=keeper))
+    for t in range(1, pairs):
+        @pl.when(pair < t)
+        def _(t=t):
+            signal(barrier, band=2 * t)
+            pl.when(hub)(lambda: signal(barrier, band=2 * t + 1))
+    from_band = jnp.where(hub, 2 * pair, pair + 1)
+    from_lev = jnp.where(lev > half, 2, jnp.where(hub, lev // half, jnp.where(lev < half - 1, 0, 2 * lev)))
+    expected = from_band + from_lev
+
+    for step in range(1, pieces):
         load(step).start()
 
     def direct(t):
@@ -89,7 +92,7 @@
     def give(step):
         where = {"band": keeper, "lev": far if step % 2 == 0 else near}
         return pltpu.make_async_remote_copy(part.at[step], inbox.at[core, step // 2, lev], part_send,
-                                            part_recv.at[core, jnp.where(lev == 0, per, step // 2)],
+                                            in_sem.at[1 + core * (per + 1) + jnp.where(lev == 0, per, step // 2)],
                                             device_id=where, device_id_type=MESH)
 
     def publish_first(c, q):
@@ -150,16 +153,15 @@
     def _():
         for q in range(per):
             inbox[1, q, lev] = part[2 * q + 1]
+        for c, q in ((1, 0), (0, 0), (0, 1), (1, 1)):
+            remote(inbox.at[c, q, pl.ds(1, n_lev - 1 - c)], part_send, in_sem.at[1 + c * (per + 1) + q]).wait_recv()
+            total = inbox[c, q, 1]
+            for e in range(2, n_lev):
+                total = total + inbox[c, q, e]
+            partial[c, q] = total
+            publish_first(c, q).start()
         for c in (1, 0):
-            for q in range(per):
-                remote(inbox.at[c, q, pl.ds(1, n_lev - 1 - c)], part_send, part_recv.at[c, q]).wait_recv()
-                total = inbox[c, q, 1]
-                for e in range(2, n_lev):
-                    total = total + inbox[c, q, e]
-                partial[c, q] = total
-                publish_first(c, q).start()
-        for c in (1, 0):
-            remote(inbox.at[c, :, 0], part_send, part_recv.at[c, per]).wait_recv()
+            remote(inbox.at[c, :, 0], part_send, in_sem.at[1 + c * (per + 1) + per]).wait_recv()
             for q in range(per):
                 total = inbox[c, q, 0] + partial[c, q]
                 outgoing[c, q] = total
@@ -270,7 +272,7 @@
             pltpu.VMEM((2, per, 2 * share + 1, lanes), f32),
             pltpu.SMEM(block_source.shape, jnp.int32), pltpu.SMEM(taper.shape, f32), pltpu.SMEM(thickness.shape, f32),
             dma((3,)), dma, dma((pieces,)),
-            flag, flag, flag, dma((n_band,)), dma((2, per + 1)), dma,
+            flag, flag, flag, dma((max(n_band, 2 * per + 3),)), dma,
         ],
         compiler_params=pltpu.CompilerParams(collective_id=0, has_side_effects=True, vmem_limit_bytes=24 << 20),
     )(*(pltpu.with_memory_space_constraint(x, pltpu.MemorySpace.HBM)

time: 16.3 us -> 15.3 us (0.939)
  Pallas kernels: 15.5 us -> 14.5 us
    pallas_call x1, Pallas kernels: 13.3 us -> 12.3 us  [body(): pl.pallas_call(functools.partial(exchange, n_band, n_lev), name='exchange...]
where the time goes in v3:
time: 15.3 us; the launch traced here: 15.1 us
  Pallas kernels  14.5 us (95%)
  between operations  0.64 us (4%)
    pallas_call x1, Pallas kernels, body(): pl.pallas_call(functools.partial(exchange, n_band, n_lev), name='exchange...  12.3 us
    pallas_call x1, Pallas kernels, body(): pl.pallas_call(write, name='write', out_shape=(jax.ShapeDtypeStruct(tend....  2.14 us

profile of v3, /device:TPU:0, one launch (start us, length us, event | category | flops | bytes accessed | tf_op | source)
XLA Modules:
  0.0 15.1 jit_solution(12336129300607229703)
XLA Ops:
  0.6 12.3 %exchange.1 = (bf16[34,512,128]{2,1,0:T(8,128)(2,1)S(1)}, f32[256,128]{1,0:T(8,128)S(1)}) custom-call(f32[128,128]{1,0:T(8,128)} %pattern.1, s32[128]{0:T(128)} %source_hbm.1, f32[34]{0:T(128)} %taper_hbm.1, f32[34]{0:T(128)} %thickness_hbm.1, bf16[34,512,128]{2,1,0:T(8,128)(2,1)} %bitcast.17), custom_call_target="tpu_custom_call" | custom-call | tf_op jit(solution)/shard_map/exchange/pallas_call | solution.py:257
  13.0 2.1 %write.1 = (bf16[34,512,128]{2,1,0:T(8,128)(2,1)}, f32[256,128]{1,0:T(8,128)}) custom-call(bf16[34,512,128]{2,1,0:T(8,128)(2,1)S(1)} %get-tuple-element.6.made, f32[256,128]{1,0:T(8,128)S(1)} %get-tuple-element.7.sums), custom_call_target="tpu_custom_call" | custom-call | tf_op jit(solution)/shard_map/write/pallas_call | solution.py:281
